TPU v7x, 128 devices: a whole 4x4x4 slice. The times are simulated.
128 devices in a mesh: layer: 8 (over y_hi, x), width: 16 (over y_lo, z, core).
Axes of the slice: x: 4, y: 4 (y_hi: 2, y_lo: 2; y = y_hi * 2 + y_lo), z: 4, core: 2. Of those that a mesh axis runs over, the one named last changes fastest.
Arguments:
- source: bfloat16 [8, 4096, 4096], P('layer', 'width'), may hold values from -6 to 6
- expand_out: bfloat16 [2560, 4096], P(None, 'width'), may hold values from -0.125 to 0.125
- expand_in: bfloat16 [2560, 4096], P(('layer', 'width')), may hold values from -0.09375 to 0.09375
- depth: float32 [16, 8], P('layer'), may hold values from -1.4 to 1.4
Outputs:
- grown: float32 [16, 2560, 2560], P('layer', 'width')
All inputs are finite; a program needn't handle non-finite values.
Results may differ from a plain program's by a relative error of at most 0.018.
Values may be sent and summed in bfloat16 or wider, within the bound.
A program may use at most 128 MiB of HBM per device.

v0:
```python
import jax
import jax.numpy as jnp
from jax import lax
from jax.sharding import Mesh
from jax.sharding import PartitionSpec as P

LAYER_WIDTH = ("layer_0", "layer_1", "width")
LAYER = ("layer_0", "layer_1")


def in_order(parts, dim):
    parts = jnp.moveaxis(parts, 0, dim)
    dims = parts.shape
    return parts.reshape(*dims[:dim], dims[dim] * dims[dim + 1], *dims[dim + 2 :])


def stacked_from(value, axes, order):
    parts = value[None]
    for k in order:
        parts = lax.all_gather(parts, axes[k], axis=0, tiled=True)
    current = [lax.axis_size(axes[k]) for k in reversed(order)]
    parts = parts.reshape(*current, *value.shape)
    turned = sorted(range(len(order)), key=lambda place: order[len(order) - 1 - place])
    return parts.transpose(*turned, *range(len(order), parts.ndim)).reshape(-1, *value.shape)


def gathered_by_axis(value, axes, order, dim):
    return in_order(stacked_from(value, axes, order), dim)


def on_device(source, expand_out, expand_in, depth):
    src_held, row_count, inner_width = source.shape
    stacked = source.reshape(src_held * row_count, inner_width)
    projected = lax.dot_general(
        stacked,
        lax.all_gather(expand_in, LAYER_WIDTH, axis=0, tiled=True),
        (((1,), (1,)), ((), ())),
        preferred_element_type=jnp.float32,
    )
    columns = projected.shape[1]
    projected = projected.astype(jnp.bfloat16).reshape(src_held, row_count, columns)
    own_rows = expand_out.shape[0] // lax.axis_size("width")
    partial_value = jnp.einsum(
        "ri,kic->rkc", expand_out, projected, preferred_element_type=jnp.float32
    ).astype(jnp.bfloat16)
    partial_value = lax.optimization_barrier(partial_value)
    summed = lax.psum_scatter(
        partial_value.astype(jnp.float32)
        .reshape(own_rows * lax.axis_size("width"), src_held * columns)
        .astype(jnp.bfloat16),
        "width",
        scatter_dimension=0,
        tiled=True,
    )
    expanded = summed.reshape(own_rows, src_held, columns)
    return jnp.einsum(
        "tm,rmc->trc",
        depth,
        gathered_by_axis(expanded, LAYER, (0, 1), 1).astype(jnp.float32),
        precision=lax.Precision.HIGHEST,
        preferred_element_type=jnp.float32,
    )


def solution(mesh):
    finer = Mesh(mesh.devices.reshape(2, 4, mesh.shape["width"]), ("layer_0", "layer_1", "width"))
    return jax.shard_map(
        on_device,
        mesh=finer,
        in_specs=(P(LAYER, "width", None), P(None, "width"), P(LAYER_WIDTH, None), P(LAYER, None)),
        out_specs=P(LAYER, "width", None),
        check_vma=False,
    )
```

profile of v0, /device:TPU:1, one launch (start us, length us, event | category | flops | bytes accessed | tf_op | source)
XLA Modules:
  0.0 518.2 jit_solution(15276849728186745125)
XLA Ops:
  6.5 0.0 copy-start
  6.5 0.0 all-gather.10.cloned.1.call-start
  6.5 0.7 all-gather.10.cloned.1.call-update
  7.3 0.0 copy-start.3
  7.3 0.0 reduce-scatter.4.cloned.1.call-start
  7.3 228.3 %all-gather.10.cloned.1.call-done = bf16[128,20,4096]{2,1,0:T(8,128)(2,1)} async-done(((bf16[1,20,4096]{2,1,0:T(8,128)(2,1)}), bf16[128,20,4096]{2,1,0:T(8,128)(2,1)}) %all-gather.10.cloned.1.call-update) | async-done | bytes 20971536 | tf_op jit(solution)/shard_map/all_gather | solution.py:36
  235.6 26.5 %reshape.25 = bf16[2560,4096]{1,0:T(8,128)(2,1)} reshape(bf16[128,20,4096]{2,1,0:T(8,128)(2,1)} %all-gather.10.cloned.1.call-done) | data formatting | bytes 41943040
  262.1 0.0 copy-done
  262.1 0.0 copy-done.3
  262.1 16.7 %fusion = bf16[2560,1,2560]{0,2,1:T(8,128)(2,1)} fusion(bf16[2560,256]{1,0:T(8,128)(2,1)S(1)} %copy-done.3, bf16[2560,4096]{1,0:T(8,128)(2,1)} %reshape.25, bf16[1,256,4096]{2,1,0:T(8,128)(2,1)S(1)} %copy-done), kind=kOutput, calls=%fused_computation.1 | convolution fusion | flops 8731361280 | bytes 37486592 | tf_op jit(solution)/shard_map/ri,kic->rkc/dot_general | solution.py:43
  278.8 17.6 %copy.14 = bf16[2560,2560]{1,0:T(8,128)(2,1)} copy(bf16[2560,2560]{0,1:T(8,128)(2,1)} %bitcast.34) | data formatting | bytes 26214400
  296.4 0.0 reduce-scatter.4.cloned.1.call-update
  296.5 0.0 all-gather.8.cloned.1.call-start
  296.5 79.2 %reduce-scatter.4.cloned.1.call-done = bf16[160,2560]{1,0:T(8,128)(2,1)} async-done(((bf16[2560,2560]{1,0:T(8,128)(2,1)}), bf16[160,2560]{1,0:T(8,128)(2,1)}) %reduce-scatter.4.cloned.1.call-update) | async-done | bytes 819216 | tf_op jit(solution)/shard_map/reduce_scatter | solution.py:47
  375.7 0.0 all-gather.8.cloned.1.call-update
  375.7 0.2 all-gather.6.cloned.1.call-start
  376.0 35.2 %all-gather.8.cloned.1.call-done = bf16[320,2560]{1,0:T(8,128)(2,1)} async-done(((bf16[160,2560]{1,0:T(8,128)(2,1)}), bf16[320,2560]{1,0:T(8,128)(2,1)}) %all-gather.8.cloned.1.call-update) | async-done | bytes 1638416 | tf_op jit(solution)/shard_map/all_gather | solution.py:20
  411.2 0.0 all-gather.6.cloned.1.call-update
  411.2 68.7 %all-gather.6.cloned.1.call-done = bf16[8,160,1,2560]{3,1,2,0:T(8,128)(2,1)} async-done(((bf16[2,160,1,2560]{3,1,2,0:T(8,128)(2,1)}), bf16[8,160,1,2560]{3,1,2,0:T(8,128)(2,1)}) %all-gather.6.cloned.1.call-update) | async-done | bytes 6553616 | tf_op jit(solution)/shard_map/all_gather | solution.py:20
  479.9 10.6 %copy.12 = bf16[2,4,160,1,2560]{4,1,0,2,3:T(4,128)(2,1)} copy(bf16[2,4,160,1,2560]{4,2,0,1,3:T(8,128)(2,1)} %bitcast.35) | data formatting | bytes 13107200 | tf_op jit(solution)/shard_map/transpose | solution.py:24
  490.5 11.4 %reshape.21 = bf16[8,160,1,2560]{3,0,1,2:T(8,128)(2,1)} reshape(bf16[2,4,160,1,2560]{4,1,0,2,3:T(4,128)(2,1)} %copy.12) | data formatting | bytes 13107200 | tf_op jit(solution)/shard_map/reshape | solution.py:24
  502.0 7.4 %fusion.3 = f32[2,160,2560]{2,0,1:T(2,128)S(1)} fusion(bf16[8,160,1,2560]{3,0,1,2:T(8,128)(2,1)} %reshape.21, f32[2,8]{1,0:T(2,128)S(1)} %copy-done.2), kind=kOutput, calls=%fused_computation.4 | convolution fusion | flops 78643200 | bytes 9830464 | tf_op jit(solution)/shard_map/tm,rmc->trc/dot_general | solution.py:56
  509.3 2.3 copy.13
  511.6 0.0 copy-done.1
  (3 shorter events, 0.0 us)
Async XLA Ops:
  6.5 255.5 %copy-start = (bf16[1,256,4096]{2,1,0:T(8,128)(2,1)S(1)}, bf16[1,256,4096]{2,1,0:T(8,128)(2,1)}, u32[]{:S(2)}) copy-start(bf16[1,256,4096]{2,1,0:T(8,128)(2,1)} %param.4) | copy-start | bytes 6291460
  6.5 229.0 %all-gather.10.cloned.1.call-start = ((), (), s32[]{:S(2)}) async-start(), calls=%async_computation.3 | async-start | bytes 25362432 | tf_op jit(solution)/shard_map/all_gather | solution.py:36
  7.3 254.8 %copy-start.3 = (bf16[2560,256]{1,0:T(8,128)(2,1)S(1)}, bf16[2560,256]{1,0:T(8,128)(2,1)}, u32[]{:S(2)}) copy-start(bf16[2560,256]{1,0:T(8,128)(2,1)} %param.5) | copy-start | bytes 3932164
  7.3 368.4 %reduce-scatter.4.cloned.1.call-start = ((), (), s32[]{:S(2)}) async-start(), calls=%async_computation.4 | async-start | bytes 13926400 | tf_op jit(solution)/shard_map/reduce_scatter | solution.py:47
  296.5 114.7 %all-gather.8.cloned.1.call-start = ((), (), s32[]{:S(2)}) async-start(), calls=%async_computation.2 | async-start | bytes 2457600 | tf_op jit(solution)/shard_map/all_gather | solution.py:20
  375.7 104.2 %all-gather.6.cloned.1.call-start = ((), (), s32[]{:S(2)}) async-start(), calls=%async_computation.1 | async-start | bytes 8192000 | tf_op jit(solution)/shard_map/all_gather | solution.py:20
  490.5 11.4 %copy-start.2 = (f32[2,8]{1,0:T(2,128)S(1)}, f32[2,8]{1,0:T(2,128)}, u32[]{:S(2)}) copy-start(f32[2,8]{1,0:T(2,128)} %param.7) | copy-start | bytes 196
  490.5 21.1 %copy-start.1 = (bf16[1,256,4096]{2,1,0:T(8,128)(2,1)S(1)}, bf16[1,256,4096]{2,1,0:T(8,128)(2,1)}, u32[]{:S(2)}) copy-start(bf16[1,256,4096]{2,1,0:T(8,128)(2,1)} %param.4) | copy-start | bytes 6291460
Sparse Core Ops, SparseCore 0:
  9.1 226.4 all-gather.9
  296.6 79.0 reduce-scatter.3
  377.4 33.7 all-gather.7
  412.7 67.1 all-gather.5
where the time goes:
time: 520 us; the launch traced here: 518 us
  waiting for transfers between devices  412 us (79%)
  local copies, waits for them, and re-layouts  68.5 us (13%)
  matrix products  24.1 us (5%)
  between operations  13.1 us (3%)
    all_gather x1, waiting for transfers between devices, on_device(): lax.all_gather(expand_in, LAYER_WIDTH, axis=0, tiled=True)  228 us
    all_gather x2, waiting for transfers between devices, stacked_from(): parts = lax.all_gather(parts, axes[k], axis=0, tiled=True)  104 us
    reduce_scatter x1, waiting for transfers between devices, on_device(): lax.psum_scatter(partial_value.astype(jnp.float32).reshape(own_rows * lax...  79.2 us
    unnamed x10, local copies, waits for them, and re-layouts  44.1 us
    dot_general x1, matrix products, on_device(): jnp.einsum('ri,kic->rkc', expand_out, projected, preferred_element_type=j...  16.7 us
    reshape x1, local copies, waits for them, and re-layouts, stacked_from(): parts.transpose(*turned, *range(len(order), parts.ndim))  11.4 us
    transpose x1, local copies, waits for them, and re-layouts, stacked_from(): parts.transpose(*turned, *range(len(order), parts.ndim))  10.6 us
  transfers between devices with their start and end apart: 4, of which 4 were waited for; matrix products, arithmetic and copies ran while one was open for 0% of the time, Pallas kernels for 0%

commit v1 on v0

--- a/solution.py
+++ b/solution.py
@@ -33,7 +33,10 @@
     stacked = source.reshape(src_held * row_count, inner_width)
     projected = lax.dot_general(
         stacked,
-        lax.all_gather(expand_in, LAYER_WIDTH, axis=0, tiled=True),
+        jnp.concatenate(
+            lax.all_to_all(jnp.stack([expand_in] * lax.axis_size(LAYER_WIDTH)), LAYER_WIDTH, 0, 0),
+            axis=0,
+        ),
         (((1,), (1,)), ((), ())),
         preferred_element_type=jnp.float32,
     )

time: 520 us -> 609 us (1.17)
  blocking collectives: 0 us -> 296 us
  waiting for transfers between devices: 412 us -> 200 us
    all_to_all x0 -> x1, blocking collectives: none -> 296 us  [on_device(): lax.all_to_all(jnp.stack([expand_in] * lax.axis_size(LAYER_WIDTH)), LAYER...]
    all_gather x1 -> x0, waiting for transfers between devices: 228 us -> none  [on_device(): lax.all_gather(expand_in, LAYER_WIDTH, axis=0, tiled=True)]
    reshape x0 -> x1, local copies, waits for them, and re-layouts: none -> 26.6 us  [on_device(): jnp.concatenate(lax.all_to_all(jnp.stack([expand_in] * lax.axis_size(LAYE...]
    unnamed x10 -> x9, local copies, waits for them, and re-layouts: 44.1 us -> 17.6 us
    reduce_scatter x1, waiting for transfers between devices: 79.2 us -> 96.2 us  [on_device(): lax.psum_scatter(partial_value.astype(jnp.float32).reshape(own_rows * lax...]
  transfers between devices with their start and end apart: 4 -> 3, of which waited for: 4 -> 3; matrix products, arithmetic and copies ran while one was open for 0% -> 0% of each run, Pallas kernels for 0% -> 0%
where the time goes in v1:
time: 609 us; the launch traced here: 607 us
  blocking collectives  296 us (49%)
  waiting for transfers between devices  200 us (33%)
  local copies, waits for them, and re-layouts  73.3 us (12%)
  matrix products  24.1 us (4%)
  between operations  13.1 us (2%)
    all_to_all x1, blocking collectives, on_device(): lax.all_to_all(jnp.stack([expand_in] * lax.axis_size(LAYER_WIDTH)), LAYER...  296 us
    all_gather x2, waiting for transfers between devices, stacked_from(): parts = lax.all_gather(parts, axes[k], axis=0, tiled=True)  104 us
    reduce_scatter x1, waiting for transfers between devices, on_device(): lax.psum_scatter(partial_value.astype(jnp.float32).reshape(own_rows * lax...  96.2 us
    reshape x1, local copies, waits for them, and re-layouts, on_device(): jnp.concatenate(lax.all_to_all(jnp.stack([expand_in] * lax.axis_size(LAYE...  26.6 us
    unnamed x9, local copies, waits for them, and re-layouts  17.6 us
    dot_general x1, matrix products, on_device(): jnp.einsum('ri,kic->rkc', expand_out, projected, preferred_element_type=j...  16.7 us
  transfers between devices with their start and end apart: 3, of which 3 were waited for; matrix products, arithmetic and copies ran while one was open for 0% of the time, Pallas kernels for 0%

profile of v1, /device:TPU:1, one launch (start us, length us, event | category | flops | bytes accessed | tf_op | source)
XLA Modules:
  0.0 607.1 jit_solution(10722201076708766691)
XLA Ops:
  6.5 0.0 copy-start
  6.5 0.0 reduce-scatter.4.cloned.1.call-start
  6.5 4.7 stack.2
  11.2 296.0 %all_to_all.5 = bf16[128,20,4096]{2,1,0:T(8,128)(2,1)} all-to-all(bf16[128,20,4096]{2,1,0:T(8,128)(2,1)S(1)} %stack.2), channel_id=1, replica_groups=mesh['layer_0'=2,'layer_1'=4,'width'=16] {'layer_0','layer_1','width'}, dimensions={0} | all-to-all | bytes 41943040 | tf_op jit(solution)/shard_map/all_to_all | solution.py:37
  307.2 0.0 copy-start.3
  307.2 26.6 %reshape.25 = bf16[2560,4096]{1,0:T(8,128)(2,1)} reshape(bf16[128,20,4096]{2,1,0:T(8,128)(2,1)} %all_to_all.5) | data formatting | bytes 41943040 | tf_op jit(solution)/shard_map/reshape | solution.py:36
  333.8 0.0 copy-done
  333.8 0.0 copy-done.3
  333.8 16.7 %fusion = bf16[2560,1,2560]{0,2,1:T(8,128)(2,1)} fusion(bf16[2560,256]{1,0:T(8,128)(2,1)S(1)} %copy-done.3, bf16[2560,4096]{1,0:T(8,128)(2,1)} %reshape.25, bf16[1,256,4096]{2,1,0:T(8,128)(2,1)S(1)} %copy-done), kind=kOutput, calls=%fused_computation.1 | convolution fusion | flops 8731361280 | bytes 37486592 | tf_op jit(solution)/shard_map/ri,kic->rkc/dot_general | solution.py:46
  350.6 17.6 %copy.14 = bf16[2560,2560]{1,0:T(8,128)(2,1)} copy(bf16[2560,2560]{0,1:T(8,128)(2,1)} %bitcast.33) | data formatting | bytes 26214400
  368.2 0.0 reduce-scatter.4.cloned.1.call-update
  368.2 0.0 all-gather.6.cloned.1.call-start
  368.3 96.2 %reduce-scatter.4.cloned.1.call-done = bf16[160,2560]{1,0:T(8,128)(2,1)} async-done(((bf16[2560,2560]{1,0:T(8,128)(2,1)}), bf16[160,2560]{1,0:T(8,128)(2,1)}) %reduce-scatter.4.cloned.1.call-update) | async-done | bytes 819216 | tf_op jit(solution)/shard_map/reduce_scatter | solution.py:50
  464.5 0.0 all-gather.6.cloned.1.call-update
  464.5 0.2 all-gather.4.cloned.1.call-start
  464.7 35.2 %all-gather.6.cloned.1.call-done = bf16[320,2560]{1,0:T(8,128)(2,1)} async-done(((bf16[160,2560]{1,0:T(8,128)(2,1)}), bf16[320,2560]{1,0:T(8,128)(2,1)}) %all-gather.6.cloned.1.call-update) | async-done | bytes 1638416 | tf_op jit(solution)/shard_map/all_gather | solution.py:20
  499.9 0.0 all-gather.4.cloned.1.call-update
  500.0 68.9 %all-gather.4.cloned.1.call-done = bf16[8,160,1,2560]{3,1,2,0:T(8,128)(2,1)} async-done(((bf16[2,160,1,2560]{3,1,2,0:T(8,128)(2,1)}), bf16[8,160,1,2560]{3,1,2,0:T(8,128)(2,1)}) %all-gather.4.cloned.1.call-update) | async-done | bytes 6553616 | tf_op jit(solution)/shard_map/all_gather | solution.py:20
  568.8 10.6 %copy.12 = bf16[2,4,160,1,2560]{4,1,0,2,3:T(4,128)(2,1)} copy(bf16[2,4,160,1,2560]{4,2,0,1,3:T(8,128)(2,1)} %bitcast.34) | data formatting | bytes 13107200 | tf_op jit(solution)/shard_map/transpose | solution.py:24
  579.5 11.4 %reshape.27 = bf16[8,160,1,2560]{3,0,1,2:T(8,128)(2,1)} reshape(bf16[2,4,160,1,2560]{4,1,0,2,3:T(4,128)(2,1)} %copy.12) | data formatting | bytes 13107200 | tf_op jit(solution)/shard_map/reshape | solution.py:24
  590.9 0.0 copy-done.2
  590.9 7.4 %fusion.3 = f32[2,160,2560]{2,0,1:T(2,128)S(1)} fusion(bf16[8,160,1,2560]{3,0,1,2:T(8,128)(2,1)} %reshape.27, f32[2,8]{1,0:T(2,128)S(1)} %copy-done.2), kind=kOutput, calls=%fused_computation.4 | convolution fusion | flops 78643200 | bytes 9830464 | tf_op jit(solution)/shard_map/tm,rmc->trc/dot_general | solution.py:59
  598.3 2.3 copy.13
  600.6 0.0 copy-done.1
  (2 shorter events, 0.0 us)
Async XLA Ops:
  6.5 327.3 %copy-start = (bf16[1,256,4096]{2,1,0:T(8,128)(2,1)S(1)}, bf16[1,256,4096]{2,1,0:T(8,128)(2,1)}, u32[]{:S(2)}) copy-start(bf16[1,256,4096]{2,1,0:T(8,128)(2,1)} %param.4) | copy-start | bytes 6291460
  6.5 457.9 %reduce-scatter.4.cloned.1.call-start = ((), (), s32[]{:S(2)}) async-start(), calls=%async_computation.4 | async-start | bytes 13926400 | tf_op jit(solution)/shard_map/reduce_scatter | solution.py:50
  307.2 26.6 %copy-start.3 = (bf16[2560,256]{1,0:T(8,128)(2,1)S(1)}, bf16[2560,256]{1,0:T(8,128)(2,1)}, u32[]{:S(2)}) copy-start(bf16[2560,256]{1,0:T(8,128)(2,1)} %param.5) | copy-start | bytes 3932164
  368.2 131.7 %all-gather.6.cloned.1.call-start = ((), (), s32[]{:S(2)}) async-start(), calls=%async_computation.3 | async-start | bytes 2457600 | tf_op jit(solution)/shard_map/all_gather | solution.py:20
  464.5 104.3 %all-gather.4.cloned.1.call-start = ((), (), s32[]{:S(2)}) async-start(), calls=%async_computation.2 | async-start | bytes 8192000 | tf_op jit(solution)/shard_map/all_gather | solution.py:20
  579.5 11.4 %copy-start.2 = (f32[2,8]{1,0:T(2,128)S(1)}, f32[2,8]{1,0:T(2,128)}, u32[]{:S(2)}) copy-start(f32[2,8]{1,0:T(2,128)} %param.7) | copy-start | bytes 196
  579.5 21.1 %copy-start.1 = (bf16[1,256,4096]{2,1,0:T(8,128)(2,1)S(1)}, bf16[1,256,4096]{2,1,0:T(8,128)(2,1)}, u32[]{:S(2)}) copy-start(bf16[1,256,4096]{2,1,0:T(8,128)(2,1)} %param.4) | copy-start | bytes 6291460
Sparse Core Ops, SparseCore 0:
  368.4 96.0 reduce-scatter.3
  466.1 33.7 all-gather.5
  501.6 67.1 all-gather.3
